TPU v7x, 32 devices: a whole 2x2x4 slice. The times are simulated.
32 devices in a mesh: mp: 8 (over z, y), rows: 4 (over x, core).
Axes of the slice: x: 2, y: 2, z: 4, core: 2. Of those that a mesh axis runs over, the one named last changes fastest.
Arguments:
- inputs: float32 [1024, 16384], P('rows', 'mp'), may hold values from -6 to 6
- weight: float32 [512, 16384], P('mp'), may hold values from -1.5 to 1.5, as said below
Outputs:
- row_scale: float32 [1024], P('rows')
- product: float32 [512, 1024], P('mp', 'rows')
- normalized: float32 [512, 1024], P('mp')
Inputs may be any that keep to these rules, and one draw needn't show every extreme that they name: A weight matrix whose rows carry different scales.
All inputs are finite; a program needn't handle non-finite values. Where the computation divides by a largest or mean magnitude, that divisor is 1e-20 or more.
Results may differ from a plain program's by a relative error of at most 0.0003.
Values may be sent and summed in bfloat16 or wider, within the bound.
A program may use at most 64 MiB of HBM per device.

v0:
```python
import jax
import jax.numpy as jnp
from jax import lax
from jax.sharding import PartitionSpec as P

epsilon = 1e-06


def split_two(values):
    scaled = values * 128.0
    first = jnp.floor(scaled)
    second = jnp.floor((scaled - first) * 256.0)
    return (first.astype(jnp.bfloat16), second.astype(jnp.bfloat16))


def matmul(w_side, x_side):
    return lax.dot_general(
        w_side, x_side, (((1,), (1,)), ((), ())), preferred_element_type=jnp.float32
    )


def pair_sums(x_parts, w_parts):
    level_zero = matmul(w_parts[0], x_parts[0])
    level_one = matmul(w_parts[0], x_parts[1]) + matmul(w_parts[1], x_parts[0])
    return (level_zero, level_one)


def combine_levels(levels):
    return levels[0] + levels[1] / 256.0


def per_device(inputs, weight):
    col_scale = jnp.max(jnp.abs(weight), axis=1) + epsilon
    w_parts = split_two(weight / col_scale[:, None])
    row_scale = lax.pmax(jnp.max(jnp.abs(inputs), axis=1), "mp") + epsilon
    x_parts = split_two(inputs / row_scale[:, None])
    stacked = jnp.stack(w_parts, axis=0)
    moved = lax.all_to_all(stacked, "mp", split_axis=2, concat_axis=1, tiled=True)
    partial_term = combine_levels(pair_sums(x_parts, (moved[0], moved[1])))
    combined = lax.psum_scatter(partial_term, "mp", scatter_dimension=0, tiled=True)
    product = combined * col_scale[:, None] * row_scale[None, :] / 16384.0
    squares = lax.psum(jnp.sum(product * product, axis=0), "mp")
    mean_square = squares / (weight.shape[0] * lax.axis_size("mp"))
    normalized = product * lax.rsqrt(mean_square + epsilon)[None, :]
    gathered_rows = lax.all_gather(normalized, "rows", axis=1, tiled=True)
    return (row_scale, product, gathered_rows)


def solution(mesh):
    return jax.shard_map(
        per_device,
        mesh=mesh,
        in_specs=(P("rows", "mp"), P("mp", None)),
        out_specs=(P("rows"), P("mp", "rows"), P("mp", None)),
        check_vma=False,
    )
```

profile of v0, /device:TPU:0, one launch (start us, length us, event | category | flops | bytes accessed | tf_op | source)
XLA Modules:
  0.0 281.4 jit_solution(13112939245431465066)
XLA Ops:
  7.2 0.0 copy-start
  7.2 2.6 abs_reduce_fusion
  9.8 0.8 copy-done
  10.6 1.1 fusion.7
  11.7 2.3 pad_maximum_fusion
  14.0 17.8 %copy.12 = bf16[2,64,16384]{1,0,2:T(2,128)(2,1)} copy(bf16[2,64,16384]{2,1,0:T(8,128)(2,1)} %pad_maximum_fusion) | data formatting | bytes 8388608 | tf_op jit(solution)/shard_map/stack | solution.py:37
  31.8 10.5 %reshape.16 = bf16[8,2,131072]{2,1,0:T(2,128)(2,1)} reshape(bf16[16384,2,64]{2,1,0:T(2,128)(2,1)} %bitcast.13) | data formatting | bytes 8388608
  42.3 0.0 copy-start.1
  42.3 7.4 %all-to-all-start = ((bf16[8,2,131072]{2,1,0:T(2,128)(2,1)}), bf16[8,2,131072]{2,1,0:T(2,128)(2,1)}, u32[]{:S(2)}, u32[]{:S(2)}) async-start(bf16[8,2,131072]{2,1,0:T(2,128)(2,1)} %reshape.16), calls=%async_computation | async-start | bytes 8388608 | tf_op jit(solution)/shard_map/all_to_all | solution.py:38
  49.7 0.0 reduce-scatter.2.cloned.1.call-start
  49.8 0.0 copy-done.1
  49.8 0.2 abs_reduce_fusion.1
  50.0 85.0 %pmax.7 = f32[256]{0:T(256)S(1)} all-reduce(f32[256]{0:T(256)S(1)} %abs_reduce_fusion.1), channel_id=1, replica_groups=mesh['mp'=8,'rows'=4] {'mp'}, use_global_device_ids=true, to_apply=%region_1.0 | all-reduce | flops 256 | bytes 2048 | tf_op jit(solution)/shard_map/pmax | solution.py:35
  135.0 0.0 copy-start.2
  135.0 8.1 %all-to-all-done = bf16[8,2,131072]{2,1,0:T(2,128)(2,1)} async-done(((bf16[8,2,131072]{2,1,0:T(2,128)(2,1)}), bf16[8,2,131072]{2,1,0:T(2,128)(2,1)}, u32[]{:S(2)}, u32[]{:S(2)}) %all-to-all-start) | async-done | bytes 4194336 | tf_op jit(solution)/shard_map/all_to_all | solution.py:38
  143.1 10.3 %reshape.17 = bf16[16384,2,64]{2,1,0:T(2,128)(2,1)} reshape(bf16[8,2,131072]{2,1,0:T(2,128)(2,1)} %all-to-all-done) | data formatting | bytes 8388608
  153.4 13.6 %copy.16 = bf16[2,64,8,2048]{3,2,1,0:T(8,128)(2,1)} copy(bf16[2,64,8,2048]{1,0,3,2:T(2,128)(2,1)} %bitcast.14) | data formatting | bytes 8388608 | tf_op jit(solution)/shard_map/all_to_all | solution.py:38
  167.0 2.7 fusion.16
  169.7 1.2 copy.14
  170.9 1.2 copy.15
  172.1 1.0 fusion.9
  173.1 0.9 fusion.8
  174.0 1.7 convolution_add_fusion.1
  175.6 0.0 reduce-scatter.2.cloned.1.call-update
  175.6 70.5 %reduce-scatter.2.cloned.1.call-done = f32[64,256]{1,0:T(8,128)} async-done(((f32[512,256]{1,0:T(8,128)}), f32[64,256]{1,0:T(8,128)}) %reduce-scatter.2.cloned.1.call-update) | async-done | bytes 65552 | tf_op jit(solution)/shard_map/reduce_scatter | solution.py:40
  246.1 1.6 multiply_reduce_fusion
  247.7 19.4 %psum.7 = f32[256]{0:T(256)S(1)} all-reduce(f32[256]{0:T(256)S(1)} %get-tuple-element.3), channel_id=1, replica_groups=mesh['mp'=8,'rows'=4] {'mp'}, use_global_device_ids=true, to_apply=%region_5.0 | all-reduce | flops 256 | bytes 2048 | tf_op jit(solution)/shard_map/psum | solution.py:42
  267.1 0.0 copy-done.2
  267.1 0.9 fusion.12
  268.0 5.8 %all_gather.3 = f32[64,1024]{1,0:T(8,128)S(1)} all-gather(f32[64,256]{1,0:T(8,128)S(1)} %fusion.12), channel_id=1, replica_groups=mesh['mp'=8,'rows'=4] {'rows'}, dimensions={1}, use_global_device_ids=true | all-gather | bytes 327680 | tf_op jit(solution)/shard_map/all_gather | solution.py:45
  273.8 0.7 copy.18
  (3 shorter events, 0.0 us)
Async XLA Ops:
  7.2 3.5 %copy-start = (f32[64,16384]{1,0:T(8,128)S(1)}, f32[64,16384]{1,0:T(8,128)}, u32[]{:S(2)}) copy-start(f32[64,16384]{1,0:T(8,128)} %param.3) | copy-start | bytes 12582916
  42.3 7.5 %copy-start.1 = (f32[256,2048]{1,0:T(8,128)S(1)}, f32[256,2048]{1,0:T(8,128)}, u32[]{:S(2)}) copy-start(f32[256,2048]{1,0:T(8,128)} %param.2) | copy-start | bytes 6291460
  42.3 100.8 %all-to-all-start = ((bf16[8,2,131072]{2,1,0:T(2,128)(2,1)}), bf16[8,2,131072]{2,1,0:T(2,128)(2,1)}, u32[]{:S(2)}, u32[]{:S(2)}) async-start(bf16[8,2,131072]{2,1,0:T(2,128)(2,1)} %reshape.16), calls=%async_computation | async-start | bytes 8388608 | tf_op jit(solution)/shard_map/all_to_all | solution.py:38
  49.7 196.4 %reduce-scatter.2.cloned.1.call-start = ((), (), s32[]{:S(2)}) async-start(), calls=%async_computation.2 | async-start | bytes 589824 | tf_op jit(solution)/shard_map/reduce_scatter | solution.py:40
  135.0 132.1 %copy-start.2 = (f32[256]{0:T(256)}, f32[256]{0:T(256)S(1)}, u32[]{:S(2)}) copy-start(f32[256]{0:T(256)S(1)} %broadcast_add_fusion) | copy-start | bytes 3076
Sparse Core Ops, SparseCore 0:
  175.8 70.3 reduce-scatter.1
where the time goes:
time: 283 us; the launch traced here: 281 us
  blocking collectives  110 us (39%)
  waiting for transfers between devices  78.6 us (28%)
  local copies, waits for them, and re-layouts  58.7 us (21%)
  between operations  14.1 us (5%)
  other arithmetic  8.76 us (3%)
  starting transfers between devices  7.48 us (3%)
  matrix products  3.54 us (1%)
    pmax x1, blocking collectives, per_device(): row_scale = lax.pmax(jnp.max(jnp.abs(inputs), axis=1), 'mp') + epsilon  85 us
    reduce_scatter x1, waiting for transfers between devices, per_device(): lax.psum_scatter(partial_term, 'mp', scatter_dimension=0, tiled=True)  70.5 us
    unnamed x9, local copies, waits for them, and re-layouts  22.3 us
    psum x1, blocking collectives, per_device(): squares = lax.psum(jnp.sum(product * product, axis=0), 'mp')  19.4 us
    another operation x1, local copies, waits for them, and re-layouts, per_device(): stacked = jnp.stack(w_parts, axis=0)  17.8 us
    all_to_all x1, local copies, waits for them, and re-layouts, per_device(): lax.all_to_all(stacked, 'mp', split_axis=2, concat_axis=1, tiled=True)  13.6 us
    all_to_all x1, waiting for transfers between devices, per_device(): lax.all_to_all(stacked, 'mp', split_axis=2, concat_axis=1, tiled=True)  8.12 us
    all_to_all x1, starting transfers between devices, per_device(): lax.all_to_all(stacked, 'mp', split_axis=2, concat_axis=1, tiled=True)  7.44 us
  transfers between devices with their start and end apart: 2, of which 2 were waited for; matrix products, arithmetic and copies ran while one was open for 0% of the time, Pallas kernels for 0%

commit v1 on v0

--- a/solution.py
+++ b/solution.py
@@ -35,7 +35,10 @@
     row_scale = lax.pmax(jnp.max(jnp.abs(inputs), axis=1), "mp") + epsilon
     x_parts = split_two(inputs / row_scale[:, None])
     stacked = jnp.stack(w_parts, axis=0)
-    moved = lax.all_to_all(stacked, "mp", split_axis=2, concat_axis=1, tiled=True)
+    moved = jnp.concatenate(
+        lax.all_to_all(jnp.stack(jnp.split(stacked, lax.axis_size("mp"), axis=2)), "mp", 0, 0),
+        axis=1,
+    )
     partial_term = combine_levels(pair_sums(x_parts, (moved[0], moved[1])))
     combined = lax.psum_scatter(partial_term, "mp", scatter_dimension=0, tiled=True)
     product = combined * col_scale[:, None] * row_scale[None, :] / 16384.0

time: 283 us -> 232 us (0.82)
  local copies, waits for them, and re-layouts: 58.7 us -> 4.22 us
  other arithmetic: 8.76 us -> 13.2 us
    unnamed x9 -> x7, local copies, waits for them, and re-layouts: 22.3 us -> 1.49 us
    another operation x1 -> x0, local copies, waits for them, and re-layouts: 17.8 us -> none  [per_device(): stacked = jnp.stack(w_parts, axis=0)]
    all_to_all x1 -> x0, local copies, waits for them, and re-layouts: 13.6 us -> none  [per_device(): lax.all_to_all(stacked, 'mp', split_axis=2, concat_axis=1, tiled=True)]
    unnamed x0 -> x7, other arithmetic: none -> 5.97 us
where the time goes in v1:
time: 232 us; the launch traced here: 231 us
  blocking collectives  110 us (47%)
  waiting for transfers between devices  78.7 us (34%)
  between operations  14.1 us (6%)
  other arithmetic  13.2 us (6%)
  starting transfers between devices  7.48 us (3%)
  local copies, waits for them, and re-layouts  4.22 us (2%)
  matrix products  3.51 us (2%)
    pmax x1, blocking collectives, per_device(): row_scale = lax.pmax(jnp.max(jnp.abs(inputs), axis=1), 'mp') + epsilon  85 us
    reduce_scatter x1, waiting for transfers between devices, per_device(): lax.psum_scatter(partial_term, 'mp', scatter_dimension=0, tiled=True)  70.6 us
    psum x1, blocking collectives, per_device(): squares = lax.psum(jnp.sum(product * product, axis=0), 'mp')  19.3 us
    all_to_all x1, waiting for transfers between devices, per_device(): lax.all_to_all(jnp.stack(jnp.split(stacked, lax.axis_size('mp'), axis=2))...  8.12 us
    all_to_all x1, starting transfers between devices, per_device(): lax.all_to_all(jnp.stack(jnp.split(stacked, lax.axis_size('mp'), axis=2))...  7.44 us
    unnamed x7, other arithmetic  5.97 us
    all_gather x1, blocking collectives, per_device(): gathered_rows = lax.all_gather(normalized, 'rows', axis=1, tiled=True)  5.78 us
  transfers between devices with their start and end apart: 2, of which 2 were waited for; matrix products, arithmetic and copies ran while one was open for 0% of the time, Pallas kernels for 0%

profile of v1, /device:TPU:0, one launch (start us, length us, event | category | flops | bytes accessed | tf_op | source)
XLA Modules:
  0.0 231.3 jit_solution(3200941102287751130)
XLA Ops:
  7.2 0.0 copy-start
  7.2 2.6 %abs_reduce_fusion = f32[64]{0:T(128)S(1)} fusion(f32[64,16384]{1,0:T(8,128)} %param.3), kind=kLoop, calls=%fused_computation.20 | loop fusion | flops 2097088 | bytes 4194560 | tf_op jit(solution)/shard_map/reduce_max | solution.py:33
  9.8 0.8 copy-done
  10.6 1.1 fusion.7
  11.7 0.8 bitcast_dynamic-update-slice_fusion.6
  12.5 0.9 bitcast_dynamic-update-slice_fusion.5
  13.4 0.9 bitcast_dynamic-update-slice_fusion.4
  14.2 0.9 bitcast_dynamic-update-slice_fusion.3
  15.1 0.9 bitcast_dynamic-update-slice_fusion.2
  16.0 0.9 bitcast_dynamic-update-slice_fusion.1
  16.8 0.8 bitcast_dynamic-update-slice_fusion
  17.7 0.9 fusion.20
  18.5 0.0 copy-start.1
  18.5 7.4 %all-to-all-start = ((bf16[8,2,64,2048]{3,2,1,0:T(8,128)(2,1)}), bf16[8,2,64,2048]{3,2,1,0:T(8,128)(2,1)}, u32[]{:S(2)}, u32[]{:S(2)}) async-start(bf16[8,2,64,2048]{3,2,1,0:T(8,128)(2,1)} %fusion.20), calls=%async_computation | async-start | bytes 8388608 | tf_op jit(solution)/shard_map/all_to_all | solution.py:39
  26.0 0.0 reduce-scatter.2.cloned.1.call-start
  26.0 0.0 copy-done.1
  26.0 0.2 abs_reduce_fusion.1
  26.2 85.0 %pmax.7 = f32[256]{0:T(256)S(1)} all-reduce(f32[256]{0:T(256)S(1)} %abs_reduce_fusion.1), channel_id=1, replica_groups=mesh['mp'=8,'rows'=4] {'mp'}, use_global_device_ids=true, to_apply=%region_1.0 | all-reduce | flops 256 | bytes 2048 | tf_op jit(solution)/shard_map/pmax | solution.py:35
  111.2 0.0 copy-start.2
  111.2 8.1 %all-to-all-done = bf16[8,2,64,2048]{3,2,1,0:T(8,128)(2,1)} async-done(((bf16[8,2,64,2048]{3,2,1,0:T(8,128)(2,1)}), bf16[8,2,64,2048]{3,2,1,0:T(8,128)(2,1)}, u32[]{:S(2)}, u32[]{:S(2)}) %all-to-all-start) | async-done | bytes 4194336 | tf_op jit(solution)/shard_map/all_to_all | solution.py:39
  119.3 2.7 %fusion.25 = (bf16[1,8,64,2048]{3,2,0,1:T(8,128)(2,1)S(1)}, bf16[1,8,64,2048]{3,2,0,1:T(8,128)(2,1)S(1)}) fusion(bf16[2,8,64,2048]{3,2,0,1:T(8,128)(2,1)} %bitcast.10), kind=kLoop, calls=%fused_computation.60 | loop fusion | bytes 8388608 | tf_op jit(solution)/shard_map/slice | solution.py:42
  122.1 1.0 fusion.9
  123.1 0.9 fusion.8
  123.9 1.7 convolution_add_fusion.1
  125.6 0.0 reduce-scatter.2.cloned.1.call-update
  125.6 70.6 %reduce-scatter.2.cloned.1.call-done = f32[64,256]{1,0:T(8,128)} async-done(((f32[512,256]{1,0:T(8,128)}), f32[64,256]{1,0:T(8,128)}) %reduce-scatter.2.cloned.1.call-update) | async-done | bytes 65552 | tf_op jit(solution)/shard_map/reduce_scatter | solution.py:43
  196.2 1.6 multiply_reduce_fusion
  197.7 19.3 %psum.7 = f32[256]{0:T(256)S(1)} all-reduce(f32[256]{0:T(256)S(1)} %get-tuple-element.3), channel_id=1, replica_groups=mesh['mp'=8,'rows'=4] {'mp'}, use_global_device_ids=true, to_apply=%region_5.0 | all-reduce | flops 256 | bytes 2048 | tf_op jit(solution)/shard_map/psum | solution.py:45
  217.1 0.0 copy-done.2
  217.1 0.9 fusion.21
  218.0 5.8 %all_gather.3 = f32[64,1024]{1,0:T(8,128)S(1)} all-gather(f32[64,256]{1,0:T(8,128)S(1)} %fusion.21), channel_id=1, replica_groups=mesh['mp'=8,'rows'=4] {'rows'}, dimensions={1}, use_global_device_ids=true | all-gather | bytes 327680 | tf_op jit(solution)/shard_map/all_gather | solution.py:48
  223.8 0.7 copy.13
  (3 shorter events, 0.0 us)
Async XLA Ops:
  7.2 3.5 %copy-start = (f32[64,16384]{1,0:T(8,128)S(1)}, f32[64,16384]{1,0:T(8,128)}, u32[]{:S(2)}) copy-start(f32[64,16384]{1,0:T(8,128)} %param.3) | copy-start | bytes 12582916
  18.5 7.5 %copy-start.1 = (f32[256,2048]{1,0:T(8,128)S(1)}, f32[256,2048]{1,0:T(8,128)}, u32[]{:S(2)}) copy-start(f32[256,2048]{1,0:T(8,128)} %param.2) | copy-start | bytes 6291460
  18.5 100.8 %all-to-all-start = ((bf16[8,2,64,2048]{3,2,1,0:T(8,128)(2,1)}), bf16[8,2,64,2048]{3,2,1,0:T(8,128)(2,1)}, u32[]{:S(2)}, u32[]{:S(2)}) async-start(bf16[8,2,64,2048]{3,2,1,0:T(8,128)(2,1)} %fusion.20), calls=%async_computation | async-start | bytes 8388608 | tf_op jit(solution)/shard_map/all_to_all | solution.py:39
  26.0 170.2 %reduce-scatter.2.cloned.1.call-start = ((), (), s32[]{:S(2)}) async-start(), calls=%async_computation.2 | async-start | bytes 589824 | tf_op jit(solution)/shard_map/reduce_scatter | solution.py:43
  111.2 105.9 %copy-start.2 = (f32[256]{0:T(256)}, f32[256]{0:T(256)S(1)}, u32[]{:S(2)}) copy-start(f32[256]{0:T(256)S(1)} %broadcast_add_fusion) | copy-start | bytes 3076
Sparse Core Ops, SparseCore 0:
  125.7 70.4 reduce-scatter.1

commit v2 on v0

--- a/solution.py
+++ b/solution.py
@@ -39,7 +39,7 @@
     partial_term = combine_levels(pair_sums(x_parts, (moved[0], moved[1])))
     combined = lax.psum_scatter(partial_term, "mp", scatter_dimension=0, tiled=True)
     product = combined * col_scale[:, None] * row_scale[None, :] / 16384.0
-    squares = lax.psum(jnp.sum(product * product, axis=0), "mp")
+    squares = jnp.sum(lax.all_gather(jnp.sum(product * product, axis=0), "mp"), axis=0)
     mean_square = squares / (weight.shape[0] * lax.axis_size("mp"))
     normalized = product * lax.rsqrt(mean_square + epsilon)[None, :]
     gathered_rows = lax.all_gather(normalized, "rows", axis=1, tiled=True)

time: 283 us -> 282 us (level)
    psum x1 -> x0, blocking collectives: 19.4 us -> none  [per_device(): squares = lax.psum(jnp.sum(product * product, axis=0), 'mp')]
    all_gather x0 -> x1, blocking collectives: none -> 18.6 us  [per_device(): lax.all_gather(jnp.sum(product * product, axis=0), 'mp')]
where the time goes in v2:
time: 282 us; the launch traced here: 281 us
  blocking collectives  109 us (39%)
  waiting for transfers between devices  78.6 us (28%)
  local copies, waits for them, and re-layouts  58.7 us (21%)
  between operations  14.1 us (5%)
  other arithmetic  8.79 us (3%)
  starting transfers between devices  7.48 us (3%)
  matrix products  3.54 us (1%)
    pmax x1, blocking collectives, per_device(): row_scale = lax.pmax(jnp.max(jnp.abs(inputs), axis=1), 'mp') + epsilon  85 us
    reduce_scatter x1, waiting for transfers between devices, per_device(): lax.psum_scatter(partial_term, 'mp', scatter_dimension=0, tiled=True)  70.5 us
    unnamed x9, local copies, waits for them, and re-layouts  22.3 us
    all_gather x1, blocking collectives, per_device(): lax.all_gather(jnp.sum(product * product, axis=0), 'mp')  18.6 us
    another operation x1, local copies, waits for them, and re-layouts, per_device(): stacked = jnp.stack(w_parts, axis=0)  17.8 us
    all_to_all x1, local copies, waits for them, and re-layouts, per_device(): lax.all_to_all(stacked, 'mp', split_axis=2, concat_axis=1, tiled=True)  13.6 us
    all_to_all x1, waiting for transfers between devices, per_device(): lax.all_to_all(stacked, 'mp', split_axis=2, concat_axis=1, tiled=True)  8.12 us
    all_to_all x1, starting transfers between devices, per_device(): lax.all_to_all(stacked, 'mp', split_axis=2, concat_axis=1, tiled=True)  7.44 us
  transfers between devices with their start and end apart: 2, of which 2 were waited for; matrix products, arithmetic and copies ran while one was open for 0% of the time, Pallas kernels for 0%

profile of v2, /device:TPU:0, one launch (start us, length us, event | category | flops | bytes accessed | tf_op | source)
XLA Modules:
  0.0 280.6 jit_solution(9002813372743664082)
XLA Ops:
  7.2 0.0 copy-start
  7.2 2.6 abs_reduce_fusion
  9.8 0.8 copy-done
  10.6 1.1 fusion.7
  11.7 2.3 pad_maximum_fusion
  14.0 17.8 %copy.12 = bf16[2,64,16384]{1,0,2:T(2,128)(2,1)} copy(bf16[2,64,16384]{2,1,0:T(8,128)(2,1)} %pad_maximum_fusion) | data formatting | bytes 8388608 | tf_op jit(solution)/shard_map/stack | solution.py:37
  31.8 10.5 %reshape.24 = bf16[8,2,131072]{2,1,0:T(2,128)(2,1)} reshape(bf16[16384,2,64]{2,1,0:T(2,128)(2,1)} %bitcast.14) | data formatting | bytes 8388608
  42.3 0.0 copy-start.1
  42.3 7.4 %all-to-all-start = ((bf16[8,2,131072]{2,1,0:T(2,128)(2,1)}), bf16[8,2,131072]{2,1,0:T(2,128)(2,1)}, u32[]{:S(2)}, u32[]{:S(2)}) async-start(bf16[8,2,131072]{2,1,0:T(2,128)(2,1)} %reshape.24), calls=%async_computation | async-start | bytes 8388608 | tf_op jit(solution)/shard_map/all_to_all | solution.py:38
  49.7 0.0 reduce-scatter.2.cloned.1.call-start
  49.8 0.0 copy-done.1
  49.8 0.2 abs_reduce_fusion.1
  50.0 85.0 %pmax.7 = f32[256]{0:T(256)S(1)} all-reduce(f32[256]{0:T(256)S(1)} %abs_reduce_fusion.1), channel_id=1, replica_groups=mesh['mp'=8,'rows'=4] {'mp'}, use_global_device_ids=true, to_apply=%region_1.0 | all-reduce | flops 256 | bytes 2048 | tf_op jit(solution)/shard_map/pmax | solution.py:35
  135.0 0.0 copy-start.2
  135.0 8.1 %all-to-all-done = bf16[8,2,131072]{2,1,0:T(2,128)(2,1)} async-done(((bf16[8,2,131072]{2,1,0:T(2,128)(2,1)}), bf16[8,2,131072]{2,1,0:T(2,128)(2,1)}, u32[]{:S(2)}, u32[]{:S(2)}) %all-to-all-start) | async-done | bytes 4194336 | tf_op jit(solution)/shard_map/all_to_all | solution.py:38
  143.1 10.3 %reshape.25 = bf16[16384,2,64]{2,1,0:T(2,128)(2,1)} reshape(bf16[8,2,131072]{2,1,0:T(2,128)(2,1)} %all-to-all-done) | data formatting | bytes 8388608
  153.4 13.6 %copy.16 = bf16[2,64,8,2048]{3,2,1,0:T(8,128)(2,1)} copy(bf16[2,64,8,2048]{1,0,3,2:T(2,128)(2,1)} %bitcast.15) | data formatting | bytes 8388608 | tf_op jit(solution)/shard_map/all_to_all | solution.py:38
  167.0 2.7 fusion.16
  169.7 1.2 copy.14
  170.9 1.2 copy.15
  172.1 1.0 fusion.9
  173.1 0.9 fusion.8
  174.0 1.7 convolution_add_fusion.1
  175.6 0.0 reduce-scatter.2.cloned.1.call-update
  175.6 70.5 %reduce-scatter.2.cloned.1.call-done = f32[64,256]{1,0:T(8,128)} async-done(((f32[512,256]{1,0:T(8,128)}), f32[64,256]{1,0:T(8,128)}) %reduce-scatter.2.cloned.1.call-update) | async-done | bytes 65552 | tf_op jit(solution)/shard_map/reduce_scatter | solution.py:40
  246.1 1.6 multiply_reduce_fusion
  247.7 18.6 %all-gather.1 = f32[8,1,256]{2,1,0:T(1,128)S(1)} all-gather(f32[1,1,256]{2,1,0:T(1,128)S(1)} %bitcast.20), channel_id=2, replica_groups=mesh['mp'=8,'rows'=4] {'mp'}, dimensions={0}, use_global_device_ids=true | all-gather | bytes 9216 | tf_op jit(solution)/shard_map/all_gather | solution.py:42
  266.3 0.0 copy-done.2
  266.3 0.9 fusion.12
  267.2 5.8 %all_gather.11 = f32[64,1024]{1,0:T(8,128)S(1)} all-gather(f32[64,256]{1,0:T(8,128)S(1)} %fusion.12), channel_id=1, replica_groups=mesh['mp'=8,'rows'=4] {'rows'}, dimensions={1}, use_global_device_ids=true | all-gather | bytes 327680 | tf_op jit(solution)/shard_map/all_gather | solution.py:45
  273.0 0.7 copy.18
  (4 shorter events, 0.0 us)
Async XLA Ops:
  7.2 3.5 %copy-start = (f32[64,16384]{1,0:T(8,128)S(1)}, f32[64,16384]{1,0:T(8,128)}, u32[]{:S(2)}) copy-start(f32[64,16384]{1,0:T(8,128)} %param.3) | copy-start | bytes 12582916
  42.3 7.5 %copy-start.1 = (f32[256,2048]{1,0:T(8,128)S(1)}, f32[256,2048]{1,0:T(8,128)}, u32[]{:S(2)}) copy-start(f32[256,2048]{1,0:T(8,128)} %param.2) | copy-start | bytes 6291460
  42.3 100.8 %all-to-all-start = ((bf16[8,2,131072]{2,1,0:T(2,128)(2,1)}), bf16[8,2,131072]{2,1,0:T(2,128)(2,1)}, u32[]{:S(2)}, u32[]{:S(2)}) async-start(bf16[8,2,131072]{2,1,0:T(2,128)(2,1)} %reshape.24), calls=%async_computation | async-start | bytes 8388608 | tf_op jit(solution)/shard_map/all_to_all | solution.py:38
  49.7 196.4 %reduce-scatter.2.cloned.1.call-start = ((), (), s32[]{:S(2)}) async-start(), calls=%async_computation.2 | async-start | bytes 589824 | tf_op jit(solution)/shard_map/reduce_scatter | solution.py:40
  135.0 131.3 %copy-start.2 = (f32[256]{0:T(256)}, f32[256]{0:T(256)S(1)}, u32[]{:S(2)}) copy-start(f32[256]{0:T(256)S(1)} %broadcast_add_fusion) | copy-start | bytes 3076
Sparse Core Ops, SparseCore 0:
  175.8 70.3 reduce-scatter.1
